TPU v7x, 128 devices: a whole 4x4x4 slice. The times are simulated.
128 devices in a mesh: dp: 4 (over x), fsdp: 8 (over y, core), enc: 4 (over z).
Axes of the slice: x: 4, y: 4, z: 4, core: 2. Of those that a mesh axis runs over, the one named last changes fastest.
Arguments:
- hidden: bfloat16 [32768, 8192], P(('dp', 'fsdp', 'enc')), may hold values from -40 to 40
- residual_gradient: bfloat16 [32768, 8192], P(('dp', 'fsdp', 'enc')), may hold values from -3 to 3
- value_output_gradient: bfloat16 [32768, 1024], P(('dp', 'fsdp', 'enc')), may hold values from -6 to 6
- attention_norm_gain: float32 [8192], replicated, may hold values from 0.1 to 1.9
- value_frozen_weight: bfloat16 [8192, 1024], P('fsdp'), may hold values from -0.0625 to 0.0625
- value_down_factor: bfloat16 [8192, 16], replicated, may hold values from -0.0625 to 0.0625
- value_up_factor: bfloat16 [16, 1024], replicated, may hold values from -0.29882812 to 0.29882812
- merger_frozen_weight: bfloat16 [5120, 8192], P(None, ('fsdp', 'enc')), may hold values from -0.078125 to 0.078125
- merger_down_factor: bfloat16 [5120, 16], replicated, may hold values from -0.078125 to 0.078125
- merger_up_factor: bfloat16 [16, 8192], P(None, ('fsdp', 'enc')), may hold values from -0.29882812 to 0.29882812
- merger_saved_preactivation: bfloat16 [4096, 5120], P(('dp', 'fsdp', 'enc')), may hold values from -5 to 5
- image_token_counts: int32 [128], P('dp'), may hold values from 8 to 16, as said below
- image_encoder_owner: int32 [128], P('dp'), may hold values from 0 to 31, as said below
- image_first_rows: int32 [128], P(('dp', 'fsdp', 'enc')), may hold values from 0 to 255, as said below
Outputs:
- layer_input_gradient: bfloat16 [32768, 8192], P(('dp', 'fsdp', 'enc'))
- preactivation_gradient: bfloat16 [4096, 5120], P(('dp', 'fsdp', 'enc'))
- value_down_gradient: float32 [8192, 16], replicated
- value_up_gradient: float32 [16, 1024], replicated
- merger_down_gradient: float32 [5120, 16], replicated
- merger_up_gradient: float32 [16, 8192], P(None, ('fsdp', 'enc'))
Inputs may be any that keep to these rules, and one draw needn't show every extreme that they name: `image_token_counts`: within each data replica some encoder device owns exactly 2 images, all of 16 visual tokens, so its rows fill all 32; no other device owns more than 2 images. `image_encoder_owner`: encoder devices are numbered within the data replica in mesh order. `image_first_rows`: images of one device lie inside its 256 rows in increasing order and don't intersect.
All inputs are finite; a program needn't handle non-finite values.
Results may differ from a plain program's by a relative error of at most 0.0085.
Values may be sent and summed in bfloat16 or wider, within the bound.
A program may use at most 192 MiB of HBM per device.

v0:
```python
import jax
import jax.numpy as jnp
from jax import lax
from jax.sharding import PartitionSpec as P

MAXIMG = 16
adapter_scale = 2.0
norm_eps = 1e-06


def laid_out(blocks, dim):
    shape = list(blocks.shape[1:])
    shape[dim] *= blocks.shape[0]
    return jnp.moveaxis(blocks, 0, dim).reshape(shape)


def sent_to_all(value, axis):
    copies = jnp.broadcast_to(value, (lax.axis_size(axis), *value.shape))
    return lax.all_to_all(copies, axis, split_axis=0, concat_axis=0, tiled=True)


def gathered_copies(value, axis, dim):
    return laid_out(sent_to_all(value, axis), dim)


def in_one_piece(arrays, axis, dim, along):
    widths = [a.shape[along] for a in arrays]
    both = jnp.concatenate(arrays, axis=along)
    out = lax.psum_scatter(both, axis, scatter_dimension=dim, tiled=True)
    return tuple(jnp.split(out, [sum(widths[:k]) for k in range(1, len(widths))], axis=along))


def over_copies(value, axis):
    return sent_to_all(value, axis).sum(axis=0)


def gelu_parts(preact):
    normal_cdf = 0.5 * (1.0 + lax.erf(preact * 0.7071067811865476))
    normal_pdf = jnp.exp(-0.5 * preact * preact) * 0.3989422804014327
    return (normal_cdf, normal_pdf)


def owner_layout(image_token_counts, image_encoder_owner, owner_count, owner_room, slot_len):
    total_images = image_token_counts.shape[0]
    image_ids = jnp.arange(total_images)
    same_owner = image_encoder_owner[:, None] == image_encoder_owner[None, :]
    earlier = image_ids[None, :] < image_ids[:, None]
    starts = jnp.sum(jnp.where(same_owner & earlier, image_token_counts[None, :], 0), axis=1)
    row_index = jnp.arange(owner_count * owner_room)
    row_owner = row_index // owner_room
    row_place = row_index % owner_room
    matches = (
        (row_owner[:, None] == image_encoder_owner[None, :])
        & (row_place[:, None] >= starts[None, :])
        & (row_place[:, None] < (starts + image_token_counts)[None, :])
    )
    source = jnp.sum(
        jnp.where(matches, image_ids[None, :] * slot_len + row_place[:, None] - starts[None, :], 0),
        axis=1,
    )
    valid_rows = jnp.any(matches, axis=1)
    return (source, valid_rows)


def take_slots(layer_input_gradient, counts_in, offsets_in):
    padded = jnp.concatenate(
        [
            layer_input_gradient,
            jnp.zeros((MAXIMG, layer_input_gradient.shape[1]), layer_input_gradient.dtype),
        ],
        axis=0,
    )
    window = lax.dynamic_slice_in_dim(padded, offsets_in[0], MAXIMG, 0)
    inside = jnp.arange(MAXIMG) < counts_in[0]
    pieces = jnp.where(inside[:, None], window, jnp.zeros_like(window))
    return pieces


def decoder_layer_block(
    incoming_rows,
    residual_input,
    value_incoming,
    attention_norm_gain,
    passed_gradient,
    value_down_factor,
    value_up_factor,
):
    values = incoming_rows.astype(jnp.float32)
    inverse = lax.rsqrt(jnp.mean(values * values, axis=1, keepdims=True) + norm_eps)
    normalized_input = (values * inverse * attention_norm_gain).astype(jnp.bfloat16)
    value_low_product = jnp.dot(
        value_incoming, value_up_factor.T, preferred_element_type=jnp.float32
    ).astype(jnp.bfloat16)
    normalized_gradient = passed_gradient.astype(jnp.float32) + adapter_scale * jnp.dot(
        value_low_product, value_down_factor.T, preferred_element_type=jnp.float32
    )
    gained = attention_norm_gain * normalized_gradient
    layer_input_gradient = (
        residual_input.astype(jnp.float32)
        + inverse * gained
        - values * inverse**3 * jnp.mean(values * gained, axis=1, keepdims=True)
    ).astype(jnp.bfloat16)
    projected_rows = jnp.dot(
        normalized_input, value_down_factor, preferred_element_type=jnp.float32
    ).astype(jnp.bfloat16)
    up_term = lax.dot_general(
        projected_rows, value_incoming, (((0,), (0,)), ((), ())), preferred_element_type=jnp.float32
    )
    down_term = lax.dot_general(
        normalized_input,
        value_low_product,
        (((0,), (0,)), ((), ())),
        preferred_element_type=jnp.float32,
    )
    return (layer_input_gradient, down_term, up_term)


def body(
    hidden,
    residual_gradient,
    value_output_gradient,
    attention_norm_gain,
    value_frozen_weight,
    value_down_factor,
    value_up_factor,
    merger_frozen_weight,
    merger_down_factor,
    merger_up_factor,
    merger_saved_preactivation,
    image_token_counts,
    image_encoder_owner,
    image_first_rows,
):
    device_total = lax.axis_size("dp") * lax.axis_size("fsdp") * lax.axis_size("enc")
    gradient_scale = 256.0 / (hidden.shape[0] * device_total)
    scale_factor = gradient_scale * adapter_scale
    owner_count = lax.axis_size("fsdp") * lax.axis_size("enc")
    owner_room = merger_saved_preactivation.shape[0]
    preact = merger_saved_preactivation.astype(jnp.float32)
    normal_cdf, normal_pdf = gelu_parts(preact)
    activation = (preact * normal_cdf).astype(jnp.bfloat16)
    act_low = jnp.dot(activation, merger_down_factor, preferred_element_type=jnp.float32).astype(
        jnp.bfloat16
    )
    all_low = gathered_copies(act_low, ("fsdp", "enc"), 0)
    columns = lax.dot_general(
        lax.all_gather(value_output_gradient, "fsdp", axis=0, tiled=True),
        value_frozen_weight,
        (((1,), (1,)), ((), ())),
        preferred_element_type=jnp.float32,
    ).astype(jnp.bfloat16)
    passed_gradient = lax.all_to_all(columns, "fsdp", split_axis=0, concat_axis=1, tiled=True)
    layer_input_gradient, down_term, up_term = decoder_layer_block(
        hidden,
        residual_gradient,
        value_output_gradient,
        attention_norm_gain,
        passed_gradient,
        value_down_factor,
        value_up_factor,
    )
    member = lax.axis_index(("fsdp", "enc"))
    local_images = image_first_rows.shape[0]
    local_counts = lax.dynamic_slice_in_dim(
        image_token_counts, member * local_images, local_images, 0
    )
    slots_out = take_slots(layer_input_gradient, local_counts, image_first_rows)
    received = lax.all_to_all(slots_out, ("fsdp", "enc"), split_axis=1, concat_axis=0, tiled=True)
    source, valid_rows = owner_layout(
        image_token_counts, image_encoder_owner, owner_count, owner_room, MAXIMG
    )
    visual_tokens = jnp.where(
        valid_rows[:, None], jnp.take(received, source, axis=0), jnp.zeros((), received.dtype)
    )
    value_partial_sum = lax.dot_general(
        visual_tokens,
        merger_frozen_weight,
        (((1,), (1,)), ((), ())),
        preferred_element_type=jnp.float32,
    )
    low_part = lax.dot_general(
        visual_tokens,
        merger_up_factor,
        (((1,), (1,)), ((), ())),
        preferred_element_type=jnp.float32,
    )
    value_partial_sum = value_partial_sum + adapter_scale * jnp.dot(
        low_part, merger_down_factor.astype(jnp.float32).T
    )
    combined_gradient, low_sum = in_one_piece((value_partial_sum, low_part), ("fsdp", "enc"), 0, 1)
    preactivation_gradient = (combined_gradient * (normal_cdf + preact * normal_pdf)).astype(
        jnp.bfloat16
    )
    term_a2 = lax.dot_general(
        activation,
        low_sum.astype(jnp.bfloat16),
        (((0,), (0,)), ((), ())),
        preferred_element_type=jnp.float32,
    )
    term_b2 = lax.dot_general(
        all_low, visual_tokens, (((0,), (0,)), ((), ())), preferred_element_type=jnp.float32
    )
    merger_up_gradient = over_copies(scale_factor * term_b2, "dp")
    value_down_gradient, value_up_gradient, merger_down_gradient = lax.psum(
        (scale_factor * down_term, scale_factor * up_term, scale_factor * term_a2),
        ("dp", "fsdp", "enc"),
    )
    return (
        layer_input_gradient,
        preactivation_gradient,
        value_down_gradient,
        value_up_gradient,
        merger_down_gradient,
        merger_up_gradient,
    )


def solution(mesh):
    placed = (
        P(("dp", "fsdp", "enc"), None),
        P(("dp", "fsdp", "enc"), None),
        P(("dp", "fsdp", "enc"), None),
        P(),
        P("fsdp", None),
        P(),
        P(),
        P(None, ("fsdp", "enc")),
        P(),
        P(None, ("fsdp", "enc")),
        P(("dp", "fsdp", "enc"), None),
        P("dp"),
        P("dp"),
        P(("dp", "fsdp", "enc")),
    )
    return jax.shard_map(
        body,
        mesh=mesh,
        in_specs=placed,
        out_specs=(
            P(("dp", "fsdp", "enc"), None),
            P(("dp", "fsdp", "enc"), None),
            P(),
            P(),
            P(),
            P(None, ("fsdp", "enc")),
        ),
        check_vma=False,
    )
```

profile of v0, /device:TPU:1, one launch (start us, length us, event | category | flops | bytes accessed | tf_op | source)
XLA Modules:
  0.0 477.0 jit_solution(13086993412335632943)
XLA Ops:
  7.2 0.0 copy-start
  7.2 0.0 all-gather.2.cloned.1.call-start
  7.2 0.7 all-gather.2.cloned.1.call-update
  7.9 37.5 %all-gather.2.cloned.1.call-done = bf16[2048,1024]{1,0:T(8,128)(2,1)} async-done(((bf16[256,1024]{1,0:T(8,128)(2,1)}), bf16[2048,1024]{1,0:T(8,128)(2,1)}) %all-gather.2.cloned.1.call-update) | async-done | bytes 4194320 | tf_op jit(solution)/shard_map/all_gather | solution.py:147
  45.4 9.4 %convolution_convert_fusion = bf16[2048,1024]{1,0:T(8,128)(2,1)} fusion(bf16[2048,1024]{1,0:T(8,128)(2,1)} %all-gather.2.cloned.1.call-done, bf16[1024,1024]{1,0:T(8,128)(2,1)} %param.18), kind=kOutput, calls=%fused_computation.21 | convolution fusion | flops 4297064448 | bytes 10485760 | tf_op jit(solution)/shard_map/dot_general | solution.py:146
  54.9 4.9 %all-to-all-start = ((bf16[8,256,1024]{2,1,0:T(8,128)(2,1)}), bf16[8,256,1024]{2,1,0:T(8,128)(2,1)}, u32[]{:S(2)}, u32[]{:S(2)}) async-start(bf16[8,256,1024]{2,1,0:T(8,128)(2,1)} %bitcast.44), calls=%async_computation | async-start | bytes 8388608 | tf_op jit(solution)/shard_map/all_to_all | solution.py:152
  60.4 0.0 copy-done.12
  60.4 0.6 dynamic_slice.6
  61.0 0.0 copy-done.11
  61.0 0.2 select_reduce_fusion.1
  61.2 0.7 iota_compare_fusion.1
  61.8 0.1 select_reduce_fusion
  62.0 0.0 copy-done.6
  62.0 0.0 copy-done.9
  62.0 0.2 convolution_convert_fusion.1
  62.2 46.3 %all-to-all-done = bf16[8,256,1024]{2,1,0:T(8,128)(2,1)} async-done(((bf16[8,256,1024]{2,1,0:T(8,128)(2,1)}), bf16[8,256,1024]{2,1,0:T(8,128)(2,1)}, u32[]{:S(2)}, u32[]{:S(2)}) %all-to-all-start) | async-done | bytes 4194336 | tf_op jit(solution)/shard_map/all_to_all | solution.py:152
  108.5 3.2 convert_bitcast_fusion
  111.7 0.0 copy-start.8
  111.8 1.7 copy.40
  113.4 0.0 copy-done.8
  113.4 0.0 copy-start.2
  113.4 0.0 copy-start.4
  113.4 4.9 %fusion.2 = (f32[256]{0:T(256)S(1)}, f32[256]{0:T(256)S(1)}, f32[256,8192]{1,0:T(8,128)S(1)}) fusion(bf16[256,8192]{1,0:T(8,128)(2,1)} %param.14, f32[256,8192]{1,0:T(8,128)S(1)} %bitcast.43, bf16[256,16]{0,1:T(8,128)(2,1)S(1)} %convolution_convert_fusion.1, bf16[8192,16]{0,1:T(8,128)(2,1)} %param.19, f32[8192]{0:T(1024)S(1)} %copy-done.8), kind=kOutput, calls=%fused_computation.11 | convolution fusion | flops 83885568 | bytes 21276672 | tf_op jit(solution)/shard_map/dot_general | solution.py:94
  118.4 3.4 fusion.5
  121.8 0.0 copy-start.3
  121.8 2.0 copy-done.3
  123.8 0.1 fusion.26
  124.0 0.7 copy.42
  124.7 6.1 %all-to-all-start.1 = ((bf16[16,32,256]{2,0,1:T(8,128)(2,1)}), bf16[16,32,256]{2,0,1:T(8,128)(2,1)S(1)}, u32[]{:S(2)}, u32[]{:S(2)}) async-start(bf16[16,32,256]{2,0,1:T(8,128)(2,1)} %bitcast.38), calls=%async_computation.1 | async-start | bytes 524288 | tf_op jit(solution)/shard_map/all_to_all | solution.py:168
  130.8 0.2 reduce-scatter.2.cloned.1.call-start
  131.1 0.1 fusion.35
  131.2 8.4 %all-to-all-done.1 = bf16[16,32,256]{2,0,1:T(8,128)(2,1)S(1)} async-done(((bf16[16,32,256]{2,0,1:T(8,128)(2,1)}), bf16[16,32,256]{2,0,1:T(8,128)(2,1)S(1)}, u32[]{:S(2)}, u32[]{:S(2)}) %all-to-all-start.1) | async-done | bytes 262176 | tf_op jit(solution)/shard_map/all_to_all | solution.py:168
  139.6 5.0 %gather_fusion = bf16[1024,256]{1,0:T(8,128)(2,1)} fusion(bf16[512,256]{1,0:T(8,128)(2,1)S(1)} %bitcast.42, s32[1024]{0:T(1024)S(1)} %broadcast_clamp_fusion), kind=kCustom, calls=%fused_computation | custom fusion | bytes 1052672 | tf_op jit(solution)/shard_map/jit(_take)/gather | solution.py:173
  144.6 1.4 select_select_fusion
  146.0 0.0 copy-done.10
  146.0 0.2 fusion.40
  146.2 8.6 %fusion.39 = f32[1024,5120]{1,0:T(8,128)} fusion(bf16[1024,256]{1,0:T(8,128)(2,1)S(1)} %select_select_fusion, bf16[5120,256]{1,0:T(8,128)(2,1)S(1)} %copy-done), kind=kOutput, calls=%fused_computation.73 | convolution fusion | flops 2684354560 | bytes 24117248 | tf_op jit(solution)/shard_map/dot_general | solution.py:175
  154.8 0.2 copy.37
  155.0 13.4 %multiply_add_fusion = f32[1024,5120]{1,0:T(8,128)} fusion(f32[1024,5120]{1,0:T(8,128)} %fusion.39, f32[1024,16]{0,1:T(8,128)S(1)} %fusion.40, bf16[5120,16]{0,1:T(8,128)(2,1)S(1)} %copy-done.7), kind=kOutput, calls=%fused_computation.2 | convolution fusion | flops 178257920 | bytes 42172416 | tf_op jit(solution)/shard_map/dot_general | solution.py:187
  168.4 15.5 %pad_maximum_fusion = f32[1024,5136]{1,0:T(8,128)} fusion(f32[1024,16]{1,0:T(8,128)S(1)} %copy.37, f32[1024,5120]{1,0:T(8,128)} %multiply_add_fusion), kind=kLoop, calls=%fused_computation.1 | loop fusion | flops 5259264 | bytes 42074112 | tf_op jit(solution)/shard_map/concatenate | solution.py:28
  183.9 0.0 reduce-scatter.2.cloned.1.call-update
  183.9 0.0 copy-start.5
  183.9 0.0 all-reduce.4.cloned.1.call-start
  184.0 0.0 copy-start.1
  184.0 4.3 convolution_multiply_fusion.1
  188.3 5.0 %convolution_multiply_fusion.3 = f32[16,1024]{1,0:T(8,128)} fusion(bf16[256,1024]{1,0:T(8,128)(2,1)} %param.16, bf16[8192,16]{0,1:T(8,128)(2,1)} %param.19, bf16[256,8192]{1,0:T(8,128)(2,1)} %param.14, f32[8192]{0:T(1024)S(1)} %copy-done.8, f32[256]{0:T(256)S(1)} %get-tuple-element.13), kind=kOutput, calls=%fused_computation.28 | convolution fusion | flops 83906560 | bytes 5080064 | tf_op jit(solution)/shard_map/dot_general | solution.py:106
  193.3 117.6 %reduce-scatter.2.cloned.1.call-done = f32[32,5136]{1,0:T(8,128)} async-done(((f32[1024,5136]{1,0:T(8,128)}), f32[32,5136]{1,0:T(8,128)}) %reduce-scatter.2.cloned.1.call-update) | async-done | bytes 657424 | tf_op jit(solution)/shard_map/reduce_scatter | solution.py:29
  310.8 0.0 copy-done.5
  310.8 2.1 fusion.24
  312.9 1.1 convolution_convert_fusion.2
  314.1 1.7 convolution_multiply_fusion.2
  315.8 0.0 all-reduce.4.cloned.1.call-update
  315.8 0.1 reshape.107
  315.9 13.6 %all_to_all.42 = bf16[32,2,256]{2,1,0:T(2,128)(2,1)S(1)} all-to-all(bf16[32,2,256]{2,1,0:T(2,128)(2,1)S(1)} %reshape.107), channel_id=1, replica_groups=mesh['dp'=4,'fsdp'=8,'enc'=4] {'fsdp','enc'}, dimensions={0} | all-to-all | bytes 65536 | tf_op jit(solution)/shard_map/all_to_all | solution.py:19
  329.5 0.1 reshape.108
  329.7 0.2 reshape.97
  329.9 0.2 convolution_multiply_fusion.4
  330.1 8.2 %all_to_all.43 = f32[4,16,256]{2,1,0:T(8,128)S(1)} all-to-all(f32[4,16,256]{2,1,0:T(8,128)S(1)} %broadcast_in_dim.81), channel_id=1, replica_groups=mesh['dp'=4,'fsdp'=8,'enc'=4] {'dp'}, dimensions={0} | all-to-all | bytes 131072 | tf_op jit(solution)/shard_map/all_to_all | solution.py:19
  338.3 0.6 reduce_sum.52
  338.9 126.5 %all-reduce.4.cloned.1.call-done = (f32[8192,16]{0,1:T(8,128)}, f32[16,1024]{1,0:T(8,128)}, f32[5120,16]{0,1:T(8,128)}) async-done(((f32[8192,16]{0,1:T(8,128)}, f32[16,1024]{1,0:T(8,128)}, f32[5120,16]{0,1:T(8,128)}), (f32[8192,16]{0,1:T(8,128)}, f32[16,1024]{1,0:T(8,128)}, f32[5120,16]{0,1:T(8,128)})) %all-reduce.4.cloned.1.call-update) | async-done | bytes 917520 | tf_op jit(solution)/shard_map/psum | solution.py:204
  465.4 1.9 copy.47
  467.3 1.5 copy.48
  468.8 1.7 copy.49
  470.5 0.0 copy-done.1
  (20 shorter events, 0.1 us)
Async XLA Ops:
  7.2 139.1 %copy-start = (bf16[5120,256]{1,0:T(8,128)(2,1)S(1)}, bf16[5120,256]{1,0:T(8,128)(2,1)}, u32[]{:S(2)}) copy-start(bf16[5120,256]{1,0:T(8,128)(2,1)} %param.21) | copy-start | bytes 7864324
  7.2 38.2 %all-gather.2.cloned.1.call-start = ((), (), s32[]{:S(2)}) async-start(), calls=%async_computation.5 | async-start | bytes 4718592 | tf_op jit(solution)/shard_map/all_gather | solution.py:147
  54.8 5.5 %copy-start.12 = (s32[32]{0:T(128)S(1)}, s32[32]{0:T(128)}, u32[]{:S(2)}) copy-start(s32[32]{0:T(128)} %param.25) | copy-start | bytes 388
  54.8 6.1 %copy-start.11 = (s32[32]{0:T(128)S(1)}, s32[32]{0:T(128)}, u32[]{:S(2)}) copy-start(s32[32]{0:T(128)} %param.26) | copy-start | bytes 388
  54.9 7.1 %copy-start.6 = (bf16[256,1024]{1,0:T(8,128)(2,1)S(1)}, bf16[256,1024]{1,0:T(8,128)(2,1)}, u32[]{:S(2)}) copy-start(bf16[256,1024]{1,0:T(8,128)(2,1)} %param.16) | copy-start | bytes 1572868
  54.9 7.2 %copy-start.9 = (bf16[16,1024]{1,0:T(8,128)(2,1)S(1)}, bf16[16,1024]{1,0:T(8,128)(2,1)}, u32[]{:S(2)}) copy-start(bf16[16,1024]{1,0:T(8,128)(2,1)} %param.20) | copy-start | bytes 98308
  54.9 53.7 %all-to-all-start = ((bf16[8,256,1024]{2,1,0:T(8,128)(2,1)}), bf16[8,256,1024]{2,1,0:T(8,128)(2,1)}, u32[]{:S(2)}, u32[]{:S(2)}) async-start(bf16[8,256,1024]{2,1,0:T(8,128)(2,1)} %bitcast.44), calls=%async_computation | async-start | bytes 8388608 | tf_op jit(solution)/shard_map/all_to_all | solution.py:152
  111.7 1.7 copy-start.8
  113.4 5.0 %copy-start.2 = (bf16[256,8192]{1,0:T(8,128)(2,1)S(1)}, bf16[256,8192]{1,0:T(8,128)(2,1)}, u32[]{:S(2)}) copy-start(bf16[256,8192]{1,0:T(8,128)(2,1)} %param.14) | copy-start | bytes 12582916
  113.4 5.0 %copy-start.4 = (bf16[256,8192]{1,0:T(8,128)(2,1)S(1)}, bf16[256,8192]{1,0:T(8,128)(2,1)}, u32[]{:S(2)}) copy-start(bf16[256,8192]{1,0:T(8,128)(2,1)} %param.15) | copy-start | bytes 12582916
  121.8 2.0 copy-start.3
  123.8 22.1 %copy-start.10 = (bf16[16,256]{1,0:T(8,128)(2,1)S(1)}, bf16[16,256]{1,0:T(8,128)(2,1)}, u32[]{:S(2)}) copy-start(bf16[16,256]{1,0:T(8,128)(2,1)} %param.23) | copy-start | bytes 24580
  124.7 14.9 %all-to-all-start.1 = ((bf16[16,32,256]{2,0,1:T(8,128)(2,1)}), bf16[16,32,256]{2,0,1:T(8,128)(2,1)S(1)}, u32[]{:S(2)}, u32[]{:S(2)}) async-start(bf16[16,32,256]{2,0,1:T(8,128)(2,1)} %bitcast.38), calls=%async_computation.1 | async-start | bytes 524288 | tf_op jit(solution)/shard_map/all_to_all | solution.py:168
  130.8 180.0 %reduce-scatter.2.cloned.1.call-start = ((), (), s32[]{:S(2)}) async-start(), calls=%async_computation.6 | async-start | bytes 22167552 | tf_op jit(solution)/shard_map/reduce_scatter | solution.py:29
  146.2 8.8 %copy-start.7 = (bf16[5120,16]{0,1:T(8,128)(2,1)S(1)}, bf16[5120,16]{0,1:T(8,128)(2,1)}, u32[]{:S(2)}) copy-start(bf16[5120,16]{0,1:T(8,128)(2,1)} %param.22) | copy-start | bytes 491524
  183.9 126.9 %copy-start.5 = (bf16[32,5120]{1,0:T(8,128)(2,1)S(1)}, bf16[32,5120]{1,0:T(8,128)(2,1)}, u32[]{:S(2)}) copy-start(bf16[32,5120]{1,0:T(8,128)(2,1)} %param.24) | copy-start | bytes 983044
  183.9 281.5 %all-reduce.4.cloned.1.call-start = ((), (), s32[]{:S(2)}) async-start(), calls=%async_computation.7 | async-start | bytes 1835008 | tf_op jit(solution)/shard_map/psum | solution.py:204
  184.0 286.5 %copy-start.1 = (bf16[5120,256]{1,0:T(8,128)(2,1)S(1)}, bf16[5120,256]{1,0:T(8,128)(2,1)}, u32[]{:S(2)}) copy-start(bf16[5120,256]{1,0:T(8,128)(2,1)} %param.21) | copy-start | bytes 7864324
Sparse Core Ops, SparseCore 0:
  9.7 35.6 all-gather.1
  184.0 126.7 reduce-scatter.1
  316.7 148.6 all-reduce.3
where the time goes:
time: 478 us; the launch traced here: 477 us
  waiting for transfers between devices  337 us (71%)
  matrix products  49.1 us (10%)
  other arithmetic  27.4 us (6%)
  blocking collectives  21.8 us (5%)
  local copies, waits for them, and re-layouts  15.8 us (3%)
  between operations  14.7 us (3%)
  starting transfers between devices  11.3 us (2%)
    psum x1, waiting for transfers between devices, body(): lax.psum((scale_factor * down_term, scale_factor * up_term, scale_factor...  127 us
    reduce_scatter x1, waiting for transfers between devices, in_one_piece(): out = lax.psum_scatter(both, axis, scatter_dimension=dim, tiled=True)  118 us
    all_to_all x1, waiting for transfers between devices, body(): lax.all_to_all(columns, 'fsdp', split_axis=0, concat_axis=1, tiled=True)  46.3 us
    all_gather x1, waiting for transfers between devices, body(): lax.all_gather(value_output_gradient, 'fsdp', axis=0, tiled=True)  37.5 us
    all_to_all x2, blocking collectives, sent_to_all(): return lax.all_to_all(copies, axis, split_axis=0, concat_axis=0, tiled=True)  21.8 us
    concatenate x1, other arithmetic, in_one_piece(): both = jnp.concatenate(arrays, axis=along)  15.5 us
    dot_general x1, matrix products, body(): jnp.dot(low_part, merger_down_factor.astype(jnp.float32).T)  13.4 us
  transfers between devices with their start and end apart: 5, of which 5 were waited for; matrix products, arithmetic and copies ran while one was open for 3% of the time, Pallas kernels for 0%

commit v1 on v0

--- a/solution.py
+++ b/solution.py
@@ -143,8 +143,11 @@
         jnp.bfloat16
     )
     all_low = gathered_copies(act_low, ("fsdp", "enc"), 0)
+    view_part = lambda xin, at_axis: jnp.concatenate(
+        lax.all_to_all(jnp.stack(lax.axis_size("fsdp") * [xin], 0), "fsdp", 0, 0), at_axis
+    )
     columns = lax.dot_general(
-        lax.all_gather(value_output_gradient, "fsdp", axis=0, tiled=True),
+        view_part(value_output_gradient, 0),
         value_frozen_weight,
         (((1,), (1,)), ((), ())),
         preferred_element_type=jnp.float32,

time: 478 us -> 495 us (1.036)
  blocking collectives: 21.8 us -> 76.3 us
  waiting for transfers between devices: 337 us -> 299 us
    all_to_all x0 -> x1, blocking collectives: none -> 54.4 us  [body(): lax.all_to_all(jnp.stack(lax.axis_size('fsdp') * [xin], 0), 'fsdp', 0, 0)]
    all_gather x1 -> x0, waiting for transfers between devices: 37.5 us -> none  [body(): lax.all_gather(value_output_gradient, 'fsdp', axis=0, tiled=True)]
  transfers between devices with their start and end apart: 5 -> 4, of which waited for: 5 -> 4; matrix products, arithmetic and copies ran while one was open for 3% -> 3% of each run, Pallas kernels for 0% -> 0%
where the time goes in v1:
time: 495 us; the launch traced here: 494 us
  waiting for transfers between devices  299 us (60%)
  blocking collectives  76.3 us (15%)
  matrix products  46.2 us (9%)
  other arithmetic  27.4 us (6%)
  local copies, waits for them, and re-layouts  17.5 us (4%)
  between operations  15 us (3%)
  starting transfers between devices  12.9 us (3%)
    psum x1, waiting for transfers between devices, body(): lax.psum((scale_factor * down_term, scale_factor * up_term, scale_factor...  126 us
    reduce_scatter x1, waiting for transfers between devices, in_one_piece(): out = lax.psum_scatter(both, axis, scatter_dimension=dim, tiled=True)  118 us
    all_to_all x1, blocking collectives, body(): lax.all_to_all(jnp.stack(lax.axis_size('fsdp') * [xin], 0), 'fsdp', 0, 0)  54.4 us
    all_to_all x1, waiting for transfers between devices, body(): lax.all_to_all(columns, 'fsdp', split_axis=0, concat_axis=1, tiled=True)  46.3 us
    all_to_all x2, blocking collectives, sent_to_all(): return lax.all_to_all(copies, axis, split_axis=0, concat_axis=0, tiled=True)  21.9 us
    concatenate x1, other arithmetic, in_one_piece(): both = jnp.concatenate(arrays, axis=along)  15.5 us
    dot_general x1, matrix products, body(): jnp.dot(low_part, merger_down_factor.astype(jnp.float32).T)  13.6 us
  transfers between devices with their start and end apart: 4, of which 4 were waited for; matrix products, arithmetic and copies ran while one was open for 3% of the time, Pallas kernels for 0%

profile of v1, /device:TPU:1, one launch (start us, length us, event | category | flops | bytes accessed | tf_op | source)
XLA Modules:
  0.0 494.0 jit_solution(8538102132644149656)
XLA Ops:
  7.2 0.0 copy-start
  7.2 0.0 copy-start.13
  7.2 1.7 stack.2
  8.9 54.4 %all_to_all.47 = bf16[8,256,1024]{2,1,0:T(8,128)(2,1)S(1)} all-to-all(bf16[8,256,1024]{2,1,0:T(8,128)(2,1)S(1)} %stack.2), channel_id=1, replica_groups=mesh['dp'=4,'fsdp'=8,'enc'=4] {'fsdp'}, dimensions={0} | all-to-all | bytes 8388608 | tf_op jit(solution)/shard_map/all_to_all | solution.py:147
  63.3 0.0 copy-done.13
  63.3 6.2 %convolution_convert_fusion = bf16[2048,1024]{1,0:T(8,128)(2,1)} fusion(bf16[2048,1024]{1,0:T(8,128)(2,1)S(1)} %bitcast.46, bf16[1024,1024]{1,0:T(8,128)(2,1)S(1)} %copy-done.13), kind=kOutput, calls=%fused_computation.21 | convolution fusion | flops 4297064448 | bytes 10485760 | tf_op jit(solution)/shard_map/dot_general | solution.py:149
  69.6 5.6 %all-to-all-start.1 = ((bf16[8,256,1024]{2,1,0:T(8,128)(2,1)}), bf16[8,256,1024]{2,1,0:T(8,128)(2,1)}, u32[]{:S(2)}, u32[]{:S(2)}) async-start(bf16[8,256,1024]{2,1,0:T(8,128)(2,1)} %bitcast.45), calls=%async_computation.1 | async-start | bytes 8388608 | tf_op jit(solution)/shard_map/all_to_all | solution.py:155
  75.8 0.0 copy-done.12
  75.9 0.6 dynamic_slice.6
  76.4 0.0 copy-done.11
  76.4 0.2 select_reduce_fusion.1
  76.7 0.7 iota_compare_fusion.1
  77.3 0.1 select_reduce_fusion
  77.5 0.0 copy-done.6
  77.5 0.0 copy-done.9
  77.5 0.2 convolution_convert_fusion.1
  77.7 46.3 %all-to-all-done.1 = bf16[8,256,1024]{2,1,0:T(8,128)(2,1)} async-done(((bf16[8,256,1024]{2,1,0:T(8,128)(2,1)}), bf16[8,256,1024]{2,1,0:T(8,128)(2,1)}, u32[]{:S(2)}, u32[]{:S(2)}) %all-to-all-start.1) | async-done | bytes 4194336 | tf_op jit(solution)/shard_map/all_to_all | solution.py:155
  124.0 3.2 convert_bitcast_fusion
  127.2 0.0 copy-start.8
  127.2 1.7 copy.40
  128.9 0.0 copy-done.8
  128.9 0.0 copy-start.2
  128.9 0.0 copy-start.4
  128.9 4.9 fusion.2
  133.9 0.0 copy-done.2
  133.9 3.4 fusion.5
  137.3 0.0 copy-start.3
  137.3 2.0 copy-done.3
  139.3 0.1 fusion.26
  139.4 0.7 copy.42
  140.2 7.0 %all-to-all-start.2 = ((bf16[16,32,256]{2,0,1:T(8,128)(2,1)}), bf16[16,32,256]{2,0,1:T(8,128)(2,1)S(1)}, u32[]{:S(2)}, u32[]{:S(2)}) async-start(bf16[16,32,256]{2,0,1:T(8,128)(2,1)} %bitcast.39), calls=%async_computation.2 | async-start | bytes 524288 | tf_op jit(solution)/shard_map/all_to_all | solution.py:171
  147.2 0.2 reduce-scatter.2.cloned.1.call-start
  147.4 0.1 fusion.35
  147.6 8.4 %all-to-all-done.2 = bf16[16,32,256]{2,0,1:T(8,128)(2,1)S(1)} async-done(((bf16[16,32,256]{2,0,1:T(8,128)(2,1)}), bf16[16,32,256]{2,0,1:T(8,128)(2,1)S(1)}, u32[]{:S(2)}, u32[]{:S(2)}) %all-to-all-start.2) | async-done | bytes 262176 | tf_op jit(solution)/shard_map/all_to_all | solution.py:171
  156.0 5.0 %gather_fusion = bf16[1024,256]{1,0:T(8,128)(2,1)} fusion(bf16[512,256]{1,0:T(8,128)(2,1)S(1)} %bitcast.43, s32[1024]{0:T(1024)S(1)} %broadcast_clamp_fusion), kind=kCustom, calls=%fused_computation | custom fusion | bytes 1052672 | tf_op jit(solution)/shard_map/jit(_take)/gather | solution.py:176
  161.0 1.4 select_select_fusion
  162.4 0.0 copy-done.10
  162.4 0.2 fusion.40
  162.6 8.7 %fusion.39 = f32[1024,5120]{1,0:T(8,128)} fusion(bf16[1024,256]{1,0:T(8,128)(2,1)S(1)} %select_select_fusion, bf16[5120,256]{1,0:T(8,128)(2,1)S(1)} %copy-done), kind=kOutput, calls=%fused_computation.73 | convolution fusion | flops 2684354560 | bytes 24117248 | tf_op jit(solution)/shard_map/dot_general | solution.py:178
  171.3 0.2 copy.37
  171.5 13.6 %multiply_add_fusion = f32[1024,5120]{1,0:T(8,128)} fusion(f32[1024,5120]{1,0:T(8,128)} %fusion.39, f32[1024,16]{0,1:T(8,128)S(1)} %fusion.40, bf16[5120,16]{0,1:T(8,128)(2,1)S(1)} %copy-done.7), kind=kOutput, calls=%fused_computation.2 | convolution fusion | flops 178257920 | bytes 42172416 | tf_op jit(solution)/shard_map/dot_general | solution.py:190
  185.1 15.5 %pad_maximum_fusion = f32[1024,5136]{1,0:T(8,128)} fusion(f32[1024,16]{1,0:T(8,128)S(1)} %copy.37, f32[1024,5120]{1,0:T(8,128)} %multiply_add_fusion), kind=kLoop, calls=%fused_computation.1 | loop fusion | flops 5259264 | bytes 42074112 | tf_op jit(solution)/shard_map/concatenate | solution.py:28
  200.6 0.0 reduce-scatter.2.cloned.1.call-update
  200.6 0.0 copy-start.5
  200.6 0.0 all-reduce.4.cloned.1.call-start
  200.7 0.0 copy-start.1
  200.7 4.3 convolution_multiply_fusion.1
  204.9 5.0 %convolution_multiply_fusion.3 = f32[16,1024]{1,0:T(8,128)} fusion(bf16[256,1024]{1,0:T(8,128)(2,1)} %param.16, bf16[8192,16]{0,1:T(8,128)(2,1)} %param.19, bf16[256,8192]{1,0:T(8,128)(2,1)} %param.14, f32[8192]{0:T(1024)S(1)} %copy-done.8, f32[256]{0:T(256)S(1)} %get-tuple-element.13), kind=kOutput, calls=%fused_computation.28 | convolution fusion | flops 83906560 | bytes 5080064 | tf_op jit(solution)/shard_map/dot_general | solution.py:106
  210.0 117.5 %reduce-scatter.2.cloned.1.call-done = f32[32,5136]{1,0:T(8,128)} async-done(((f32[1024,5136]{1,0:T(8,128)}), f32[32,5136]{1,0:T(8,128)}) %reduce-scatter.2.cloned.1.call-update) | async-done | bytes 657424 | tf_op jit(solution)/shard_map/reduce_scatter | solution.py:29
  327.5 2.1 fusion.24
  329.6 1.1 convolution_convert_fusion.2
  330.7 1.7 convolution_multiply_fusion.2
  332.4 0.0 all-reduce.4.cloned.1.call-update
  332.4 0.1 reshape.113
  332.6 13.6 %all_to_all.48 = bf16[32,2,256]{2,1,0:T(2,128)(2,1)S(1)} all-to-all(bf16[32,2,256]{2,1,0:T(2,128)(2,1)S(1)} %reshape.113), channel_id=1, replica_groups=mesh['dp'=4,'fsdp'=8,'enc'=4] {'fsdp','enc'}, dimensions={0} | all-to-all | bytes 65536 | tf_op jit(solution)/shard_map/all_to_all | solution.py:19
  346.2 0.1 reshape.114
  346.4 0.2 reshape.103
  346.5 0.2 convolution_multiply_fusion.4
  346.7 8.2 %all_to_all.49 = f32[4,16,256]{2,1,0:T(8,128)S(1)} all-to-all(f32[4,16,256]{2,1,0:T(8,128)S(1)} %broadcast_in_dim.81), channel_id=1, replica_groups=mesh['dp'=4,'fsdp'=8,'enc'=4] {'dp'}, dimensions={0} | all-to-all | bytes 131072 | tf_op jit(solution)/shard_map/all_to_all | solution.py:19
  355.0 0.6 reduce_sum.52
  355.6 126.5 %all-reduce.4.cloned.1.call-done = (f32[8192,16]{0,1:T(8,128)}, f32[16,1024]{1,0:T(8,128)}, f32[5120,16]{0,1:T(8,128)}) async-done(((f32[8192,16]{0,1:T(8,128)}, f32[16,1024]{1,0:T(8,128)}, f32[5120,16]{0,1:T(8,128)}), (f32[8192,16]{0,1:T(8,128)}, f32[16,1024]{1,0:T(8,128)}, f32[5120,16]{0,1:T(8,128)})) %all-reduce.4.cloned.1.call-update) | async-done | bytes 917520 | tf_op jit(solution)/shard_map/psum | solution.py:207
  482.1 1.9 copy.47
  483.9 1.5 copy.48
  485.4 1.7 copy.49
  (21 shorter events, 0.1 us)
Async XLA Ops:
  7.2 155.4 %copy-start = (bf16[5120,256]{1,0:T(8,128)(2,1)S(1)}, bf16[5120,256]{1,0:T(8,128)(2,1)}, u32[]{:S(2)}) copy-start(bf16[5120,256]{1,0:T(8,128)(2,1)} %param.21) | copy-start | bytes 7864324
  7.2 56.1 %copy-start.13 = (bf16[1024,1024]{1,0:T(8,128)(2,1)S(1)}, bf16[1024,1024]{1,0:T(8,128)(2,1)}, u32[]{:S(2)}) copy-start(bf16[1024,1024]{1,0:T(8,128)(2,1)} %param.18) | copy-start | bytes 6291460
  69.6 6.3 %copy-start.12 = (s32[32]{0:T(128)S(1)}, s32[32]{0:T(128)}, u32[]{:S(2)}) copy-start(s32[32]{0:T(128)} %param.25) | copy-start | bytes 388
  69.6 6.9 %copy-start.11 = (s32[32]{0:T(128)S(1)}, s32[32]{0:T(128)}, u32[]{:S(2)}) copy-start(s32[32]{0:T(128)} %param.26) | copy-start | bytes 388
  69.6 7.9 %copy-start.6 = (bf16[256,1024]{1,0:T(8,128)(2,1)S(1)}, bf16[256,1024]{1,0:T(8,128)(2,1)}, u32[]{:S(2)}) copy-start(bf16[256,1024]{1,0:T(8,128)(2,1)} %param.16) | copy-start | bytes 1572868
  69.6 7.9 %copy-start.9 = (bf16[16,1024]{1,0:T(8,128)(2,1)S(1)}, bf16[16,1024]{1,0:T(8,128)(2,1)}, u32[]{:S(2)}) copy-start(bf16[16,1024]{1,0:T(8,128)(2,1)} %param.20) | copy-start | bytes 98308
  69.6 54.4 %all-to-all-start.1 = ((bf16[8,256,1024]{2,1,0:T(8,128)(2,1)}), bf16[8,256,1024]{2,1,0:T(8,128)(2,1)}, u32[]{:S(2)}, u32[]{:S(2)}) async-start(bf16[8,256,1024]{2,1,0:T(8,128)(2,1)} %bitcast.45), calls=%async_computation.1 | async-start | bytes 8388608 | tf_op jit(solution)/shard_map/all_to_all | solution.py:155
  127.2 1.7 copy-start.8
  128.9 5.0 %copy-start.2 = (bf16[256,8192]{1,0:T(8,128)(2,1)S(1)}, bf16[256,8192]{1,0:T(8,128)(2,1)}, u32[]{:S(2)}) copy-start(bf16[256,8192]{1,0:T(8,128)(2,1)} %param.14) | copy-start | bytes 12582916
  128.9 5.0 %copy-start.4 = (bf16[256,8192]{1,0:T(8,128)(2,1)S(1)}, bf16[256,8192]{1,0:T(8,128)(2,1)}, u32[]{:S(2)}) copy-start(bf16[256,8192]{1,0:T(8,128)(2,1)} %param.15) | copy-start | bytes 12582916
  137.3 2.0 copy-start.3
  139.3 23.0 %copy-start.10 = (bf16[16,256]{1,0:T(8,128)(2,1)S(1)}, bf16[16,256]{1,0:T(8,128)(2,1)}, u32[]{:S(2)}) copy-start(bf16[16,256]{1,0:T(8,128)(2,1)} %param.23) | copy-start | bytes 24580
  140.2 15.8 %all-to-all-start.2 = ((bf16[16,32,256]{2,0,1:T(8,128)(2,1)}), bf16[16,32,256]{2,0,1:T(8,128)(2,1)S(1)}, u32[]{:S(2)}, u32[]{:S(2)}) async-start(bf16[16,32,256]{2,0,1:T(8,128)(2,1)} %bitcast.39), calls=%async_computation.2 | async-start | bytes 524288 | tf_op jit(solution)/shard_map/all_to_all | solution.py:171
  147.2 180.3 %reduce-scatter.2.cloned.1.call-start = ((), (), s32[]{:S(2)}) async-start(), calls=%async_computation.6 | async-start | bytes 22167552 | tf_op jit(solution)/shard_map/reduce_scatter | solution.py:29
  162.6 8.9 %copy-start.7 = (bf16[5120,16]{0,1:T(8,128)(2,1)S(1)}, bf16[5120,16]{0,1:T(8,128)(2,1)}, u32[]{:S(2)}) copy-start(bf16[5120,16]{0,1:T(8,128)(2,1)} %param.22) | copy-start | bytes 491524
  200.6 126.9 %copy-start.5 = (bf16[32,5120]{1,0:T(8,128)(2,1)S(1)}, bf16[32,5120]{1,0:T(8,128)(2,1)}, u32[]{:S(2)}) copy-start(bf16[32,5120]{1,0:T(8,128)(2,1)} %param.24) | copy-start | bytes 983044
  200.6 281.5 %all-reduce.4.cloned.1.call-start = ((), (), s32[]{:S(2)}) async-start(), calls=%async_computation.7 | async-start | bytes 1835008 | tf_op jit(solution)/shard_map/psum | solution.py:207
  200.7 286.5 %copy-start.1 = (bf16[5120,256]{1,0:T(8,128)(2,1)S(1)}, bf16[5120,256]{1,0:T(8,128)(2,1)}, u32[]{:S(2)}) copy-start(bf16[5120,256]{1,0:T(8,128)(2,1)} %param.21) | copy-start | bytes 7864324
Sparse Core Ops, SparseCore 0:
  200.7 126.7 reduce-scatter.1
  333.3 148.7 all-reduce.3
